TPU v7x, 32 devices: a whole 2x2x4 slice. The times are simulated.
32 devices in a mesh: rep: 8 (over y, x, core), row: 2 (over z_hi), col: 2 (over z_lo).
Axes of the slice: x: 2, y: 2, z: 4 (z_hi: 2, z_lo: 2; z = z_hi * 2 + z_lo), core: 2. Of those that a mesh axis runs over, the one named last changes fastest.
Arguments:
- activations: bfloat16 [2048, 2048], P(('rep', 'row'), 'col'), may hold values from -6 to 6
- out_grads: bfloat16 [2048, 2304], P(('rep', 'col'), 'row'), may hold values from -0.375 to 0.375
- error_buffer: float32 [16384, 2304], P(('rep', 'col'), 'row'), may hold values from -6 to 6
- right_factor: float32 [2304, 16], P('row'), may hold values from -6 to 6
Outputs:
- new_error: float32 [16384, 2304], P(('rep', 'col'), 'row')
- new_right: float32 [2304, 16], P('row')
All inputs are finite; a program needn't handle non-finite values.
Results may differ from a plain program's by a relative error of at most 0.0003.
Values may be sent and summed in bfloat16 or wider, within the bound.
A program may use at most 64 MiB of HBM per device.

v0:
```python
import jax
import jax.numpy as jnp
from jax import lax
from jax.sharding import PartitionSpec as P


def body(activations, out_grads, error_buffer, right_factor):
    highest = lax.Precision.HIGHEST
    gathered_acts = lax.all_gather(activations, "row", axis=0, tiled=True)
    gathered_grads = lax.all_gather(out_grads, "col", axis=0, tiled=True)
    product = lax.dot_general(
        gathered_acts, gathered_grads, (((0,), (0,)), ((), ())), preferred_element_type=jnp.float32
    )
    target = product + error_buffer
    replicas = lax.axis_size("rep")
    block = target
    left_part = lax.psum_scatter(
        jnp.dot(block, right_factor, precision=highest), "rep", scatter_dimension=0, tiled=True
    )
    left_part = lax.psum(left_part, "row")
    gram = lax.psum(jnp.dot(left_part.T, left_part, precision=highest), ("rep", "col"))
    lower = jnp.linalg.cholesky(gram)
    orth_part = jax.scipy.linalg.solve_triangular(lower, left_part.T, lower=True).T
    left_orth = lax.all_gather(orth_part, "rep", axis=0, tiled=True)
    block = target
    right_part = lax.psum_scatter(
        lax.dot_general(
            block,
            left_orth,
            (((0,), (0,)), ((), ())),
            precision=highest,
            preferred_element_type=jnp.float32,
        ),
        "rep",
        scatter_dimension=0,
        tiled=True,
    )
    right_part = lax.psum(right_part, "col") / replicas
    new_right = lax.all_gather(right_part, "rep", axis=0, tiled=True)
    approx = jnp.dot(left_orth, new_right.T, precision=highest)
    return (target - approx, new_right)


def solution(mesh):
    return jax.shard_map(
        body,
        mesh=mesh,
        in_specs=(
            P(("rep", "row"), "col"),
            P(("rep", "col"), "row"),
            P(("rep", "col"), "row"),
            P("row", None),
        ),
        out_specs=(P(("rep", "col"), "row"), P("row", None)),
        check_vma=False,
    )
```

profile of v0, /device:TPU:0, one launch (start us, length us, event | category | flops | bytes accessed | tf_op | source)
XLA Modules:
  0.0 201.1 jit_solution(1618324302884210553)
XLA Ops:
  7.2 0.0 copy-start
  7.2 0.0 reduce-scatter.5.cloned.1.call-start
  7.2 16.9 %all_gather.12 = bf16[256,1024]{1,0:T(8,128)(2,1)S(1)} all-gather(bf16[128,1024]{1,0:T(8,128)(2,1)} %param.4), channel_id=1, replica_groups=mesh['rep'=8,'row'=2,'col'=2] {'row'}, dimensions={0}, use_global_device_ids=true | all-gather | bytes 786432 | tf_op jit(solution)/shard_map/all_gather | solution.py:9
  24.1 9.0 %all_gather.13 = bf16[256,1152]{1,0:T(8,128)(2,1)S(1)} all-gather(bf16[128,1152]{1,0:T(8,128)(2,1)} %param.5), channel_id=1, replica_groups=mesh['rep'=8,'row'=2,'col'=2] {'col'}, dimensions={0}, use_global_device_ids=true | all-gather | bytes 884736 | tf_op jit(solution)/shard_map/all_gather | solution.py:10
  33.2 3.2 %convolution_add_fusion = f32[1024,1152]{1,0:T(8,128)S(1)} fusion(f32[1024,1152]{1,0:T(8,128)} %param.6, bf16[256,1024]{1,0:T(8,128)(2,1)S(1)} %all_gather.12, bf16[256,1152]{1,0:T(8,128)(2,1)S(1)} %all_gather.13), kind=kOutput, calls=%fused_computation | convolution fusion | flops 605159424 | bytes 10551296 | tf_op jit(solution)/shard_map/dot_general | solution.py:11
  36.4 0.0 copy-start.1
  36.4 2.2 %copy-done.1 = f32[1024,1152]{1,0:T(8,128)} copy-done((f32[1024,1152]{1,0:T(8,128)}, f32[1024,1152]{1,0:T(8,128)S(1)}, u32[]{:S(2)}) %copy-start.1) | copy-done | bytes 4718616
  38.6 0.0 copy-done
  38.6 4.7 %fusion.4 = f32[1024,16]{0,1:T(8,128)} fusion(f32[1024,1152]{1,0:T(8,128)S(1)} %convolution_add_fusion, f32[1152,16]{0,1:T(8,128)S(1)} %copy-done), kind=kOutput, calls=%fused_computation.13 | convolution fusion | flops 226492416 | bytes 4857856 | tf_op jit(solution)/shard_map/dot_general | solution.py:18
  43.3 0.0 reduce-scatter.5.cloned.1.call-update
  43.3 0.0 reduce-scatter.7.cloned.1.call-start
  43.4 33.4 %reduce-scatter.5.cloned.1.call-done = f32[128,16]{0,1:T(8,128)} async-done(((f32[1024,16]{0,1:T(8,128)}), f32[128,16]{0,1:T(8,128)}) %reduce-scatter.5.cloned.1.call-update) | async-done | bytes 8208 | tf_op jit(solution)/shard_map/reduce_scatter | solution.py:17
  76.7 6.0 %psum.21 = f32[128,16]{0,1:T(8,128)S(1)} all-reduce(f32[128,16]{0,1:T(8,128)} %reduce-scatter.5.cloned.1.call-done), channel_id=1, replica_groups=mesh['rep'=8,'row'=2,'col'=2] {'row'}, use_global_device_ids=true, to_apply=%region_1.0 | all-reduce | flops 2048 | bytes 16384 | tf_op jit(solution)/shard_map/psum | solution.py:20
  82.7 0.1 fusion.5
  82.8 28.3 %psum.22 = f32[16,16]{0,1:T(8,128)S(1)} all-reduce(f32[16,16]{0,1:T(8,128)S(1)} %fusion.5), channel_id=1, replica_groups=mesh['rep'=8,'row'=2,'col'=2] {'rep','col'}, use_global_device_ids=true, to_apply=%region_2.0 | all-reduce | flops 256 | bytes 2048 | tf_op jit(solution)/shard_map/psum | solution.py:21
  111.1 0.1 copy.12
  111.2 1.5 cholesky.16
  112.7 0.6 compare_reduce_fusion
  113.3 0.6 fusion
  114.0 1.2 custom-call.7
  115.2 0.2 fusion.1
  115.4 9.1 %all_gather.14 = f32[1024,16]{0,1:T(8,128)S(1)} all-gather(f32[128,16]{0,1:T(8,128)S(1)} %fusion.1), channel_id=1, replica_groups=mesh['rep'=8,'row'=2,'col'=2] {'rep'}, dimensions={0}, use_global_device_ids=true | all-gather | bytes 73728 | tf_op jit(solution)/shard_map/all_gather | solution.py:24
  124.5 10.2 %fusion.6 = f32[1152,16]{1,0:T(8,128)} fusion(f32[1024,1152]{1,0:T(8,128)} %copy-done.1, f32[1024,16]{0,1:T(8,128)S(1)} %all_gather.14), kind=kOutput, calls=%fused_computation.15 | convolution fusion | flops 226492416 | bytes 4857856
  134.6 0.0 reduce-scatter.7.cloned.1.call-update
  134.7 33.7 %reduce-scatter.7.cloned.1.call-done = f32[144,16]{1,0:T(8,128)} async-done(((f32[1152,16]{1,0:T(8,128)}), f32[144,16]{1,0:T(8,128)}) %reduce-scatter.7.cloned.1.call-update) | async-done | bytes 9232
  168.3 0.9 copy.16
  169.3 8.2 %psum.23 = f32[144,16]{0,1:T(8,128)S(1)} all-reduce(f32[144,16]{0,1:T(8,128)S(1)} %copy.16), channel_id=1, replica_groups=mesh['rep'=8,'row'=2,'col'=2] {'col'}, use_global_device_ids=true, to_apply=%region_6.7 | all-reduce | flops 2304 | bytes 18432 | tf_op jit(solution)/shard_map/psum | solution.py:38
  177.4 9.3 %all-gather = f32[8,144,16]{1,2,0:T(8,128)S(1)} all-gather(f32[1,144,16]{1,2,0:T(8,128)S(1)} %multiply_bitcast_fusion), channel_id=1, replica_groups=mesh['rep'=8,'row'=2,'col'=2] {'rep'}, dimensions={0}, use_global_device_ids=true | all-gather | bytes 82944 | tf_op jit(solution)/shard_map/all_gather | solution.py:39
  186.8 0.1 copy.13
  186.9 0.1 reshape.15
  187.0 0.0 copy-start.2
  187.0 7.2 %convolution_subtract_fusion = f32[1024,1152]{1,0:T(8,128)} fusion(f32[1024,1152]{1,0:T(8,128)} %copy-done.1, f32[1024,16]{0,1:T(8,128)S(1)} %all_gather.14, f32[1152,16]{0,1:T(8,128)S(1)} %reshape.15), kind=kOutput, calls=%fused_computation.1 | convolution fusion | flops 227672064 | bytes 9576448 | tf_op jit(solution)/shard_map/dot_general | solution.py:40
  194.2 0.0 copy-done.2
  (3 shorter events, 0.0 us)
Async XLA Ops:
  7.2 31.4 %copy-start = (f32[1152,16]{0,1:T(8,128)S(1)}, f32[1152,16]{0,1:T(8,128)}, u32[]{:S(2)}) copy-start(f32[1152,16]{0,1:T(8,128)} %param.7) | copy-start | bytes 221188
  7.2 69.5 %reduce-scatter.5.cloned.1.call-start = ((), (), s32[]{:S(2)}) async-start(), calls=%async_computation.2 | async-start | bytes 73728 | tf_op jit(solution)/shard_map/reduce_scatter | solution.py:17
  36.4 2.2 %copy-start.1 = (f32[1024,1152]{1,0:T(8,128)}, f32[1024,1152]{1,0:T(8,128)S(1)}, u32[]{:S(2)}) copy-start(f32[1024,1152]{1,0:T(8,128)S(1)} %convolution_add_fusion) | copy-start | bytes 14155780
  43.3 125.0 %reduce-scatter.7.cloned.1.call-start = ((), (), s32[]{:S(2)}) async-start(), calls=%async_computation.3 | async-start | bytes 663552
  187.0 7.2 %copy-start.2 = (f32[1152,16]{0,1:T(8,128)}, f32[1152,16]{0,1:T(8,128)S(1)}, u32[]{:S(2)}) copy-start(f32[1152,16]{0,1:T(8,128)S(1)} %reshape.15) | copy-start | bytes 221188
Sparse Core Ops, SparseCore 0:
  43.4 33.2 reduce-scatter.4
  134.8 33.5 reduce-scatter.6
where the time goes:
time: 201 us
  blocking collectives  86.8 us (43%)
  waiting for transfers between devices  67.1 us (33%)
  matrix products  25.6 us (13%)
  between operations  14.1 us (7%)
  other arithmetic  4.02 us (2%)
  local copies, waits for them, and re-layouts  3.4 us (2%)
    unnamed x3, waiting for transfers between devices  33.7 us
    reduce_scatter x1, waiting for transfers between devices, body(): lax.psum_scatter(jnp.dot(block, right_factor, precision=highest), 'rep',...  33.4 us
    psum x1, blocking collectives, body(): lax.psum(jnp.dot(left_part.T, left_part, precision=highest), ('rep', 'col'))  28.3 us
    all_gather x1, blocking collectives, body(): gathered_acts = lax.all_gather(activations, 'row', axis=0, tiled=True)  16.9 us
    unnamed x1, matrix products  10.2 us
    all_gather x1, blocking collectives, body(): new_right = lax.all_gather(right_part, 'rep', axis=0, tiled=True)  9.34 us
    all_gather x1, blocking collectives, body(): left_orth = lax.all_gather(orth_part, 'rep', axis=0, tiled=True)  9.05 us
    all_gather x1, blocking collectives, body(): gathered_grads = lax.all_gather(out_grads, 'col', axis=0, tiled=True)  9.04 us
  transfers between devices with their start and end apart: 2, of which 2 were waited for; matrix products, arithmetic and copies ran while one was open for 0% of the time, Pallas kernels for 0%

commit v1 on v0

v1 whole, which is shorter than its diff:
```python
import functools

import jax
import jax.numpy as jnp
from jax import lax
from jax.experimental import pallas as pl
from jax.experimental.pallas import tpu as pltpu
from jax.sharding import PartitionSpec as P

MESH = pl.DeviceIdType.MESH
F32 = jnp.float32
BF16 = jnp.bfloat16
LANES = 128
SUB = 8
CHUNKS = 4


def plain_body(activations, out_grads, error_buffer, right_factor):
    highest = lax.Precision.HIGHEST
    gathered_acts = lax.all_gather(activations, "row", axis=0, tiled=True)
    gathered_grads = lax.all_gather(out_grads, "col", axis=0, tiled=True)
    product = lax.dot_general(
        gathered_acts, gathered_grads, (((0,), (0,)), ((), ())), preferred_element_type=F32
    )
    target = product + error_buffer
    replicas = lax.axis_size("rep")
    left_part = lax.psum_scatter(
        jnp.dot(target, right_factor, precision=highest), "rep", scatter_dimension=0, tiled=True
    )
    left_part = lax.psum(left_part, "row")
    gram = lax.psum(jnp.dot(left_part.T, left_part, precision=highest), ("rep", "col"))
    lower = jnp.linalg.cholesky(gram)
    orth_part = jax.scipy.linalg.solve_triangular(lower, left_part.T, lower=True).T
    left_orth = lax.all_gather(orth_part, "rep", axis=0, tiled=True)
    right_part = lax.psum_scatter(
        lax.dot_general(
            target, left_orth, (((0,), (0,)), ((), ())), precision=highest, preferred_element_type=F32
        ),
        "rep",
        scatter_dimension=0,
        tiled=True,
    )
    right_part = lax.psum(right_part, "col") / replicas
    new_right = lax.all_gather(right_part, "rep", axis=0, tiled=True)
    approx = jnp.dot(left_orth, new_right.T, precision=highest)
    return (target - approx, new_right)


def split2(x):
    hi = x.astype(BF16)
    lo = (x - hi.astype(F32)).astype(BF16)
    return hi, lo


def dot(a, b, ca, cb, precision=None):
    return lax.dot_general(a, b, (((ca,), (cb,)), ((), ())), preferred_element_type=F32, precision=precision)


def factor_kernel(
    nrep, nrow, ncol, owners, tpd,
    acts, grads, err, right,
    t_out, los, nrs, nrt,
    e_buf, t_hi, t_lo, a_all, g_all, gr_own, gr_all,
    lp, l_rx, l_own, l_row, lag, gram_all, w_tx, w_rx, w_own, w_col, wag,
    esem, tsem, loc_sem, a_ss, a_rs, g_ss, g_rs, gr_ss, gr_rs,
    l_ss, l_rs, lr_ss, lr_rs, la_ss, la_rs, gm_ss, gm_rs,
    w_ss, w_rs, wc_ss, wc_rs, wa_ss, wa_rs,
):
    rep, row, col = lax.axis_index("rep"), lax.axis_index("row"), lax.axis_index("col")
    rows, cols = e_buf.shape
    rank = right.shape[1]
    chunk = rows // CHUNKS
    highest = lax.Precision.HIGHEST
    sent = []

    def remote(src, dst, ss, rs, where):
        return pltpu.make_async_remote_copy(
            src_ref=src, dst_ref=dst, send_sem=ss, recv_sem=rs, device_id=where, device_id_type=MESH
        )

    def turn(i, k, n):
        return lax.rem(i + k, n)

    barrier = pltpu.get_barrier_semaphore()
    for k in range(1, nrep):
        pl.semaphore_signal(barrier, inc=1, device_id={"rep": turn(rep, k, nrep)}, device_id_type=MESH)
    for i in range(nrow):
        for j in range(ncol):
            if i or j:
                pl.semaphore_signal(
                    barrier, inc=1,
                    device_id={"row": turn(row, i, nrow), "col": turn(col, j, ncol)},
                    device_id_type=MESH,
                )

    loads = []
    for c in range(CHUNKS):
        part = pl.ds(c * chunk, chunk)
        loads.append(pltpu.make_async_copy(err.at[part], e_buf.at[part], esem.at[c]))
        loads[-1].start()
    own_a = pltpu.make_async_copy(acts, a_all.at[row], loc_sem.at[0])
    own_g = pltpu.make_async_copy(grads, g_all.at[col], loc_sem.at[1])
    own_a.start()
    own_g.start()

    right_t = right[...].T
    r_hi, r_lo = split2(right_t)
    r_two = jnp.concatenate([r_hi, r_lo], axis=0)
    gr2 = dot(r_two, grads[...], 1, 1)
    gr_own[...] = gr2[:rank] + gr2[rank:]

    pl.semaphore_wait(barrier, nrep - 1 + nrow * ncol - 1)

    gr_copies = []
    for j in range(ncol):
        cp = remote(gr_own, gr_all.at[row], gr_ss.at[j], gr_rs.at[row], {"row": col, "col": j})
        is_self = jnp.logical_and(row == col, col == j)
        gr_copies.append((cp, is_self))

        @pl.when(jnp.logical_not(is_self))
        def _():
            cp.start()

    @pl.when(row == col)
    def _():
        gr_all[row] = gr_own[...]

    ta, tg = acts.shape[0] // 2, grads.shape[0] // 2
    bulk = []
    for half in range(2):
        part = []
        for k in range(1, nrow):
            s = pl.ds(half * ta, ta)
            part.append(remote(acts.at[s], a_all.at[row, s], a_ss.at[half, k], a_rs.at[half, k], {"row": turn(row, k, nrow)}))
        for k in range(1, ncol):
            s = pl.ds(half * tg, tg)
            part.append(remote(grads.at[s], g_all.at[col, s], g_ss.at[half, k], g_rs.at[half, k], {"col": turn(col, k, ncol)}))
        bulk.append(part)
    for cp in bulk[0]:
        cp.start()

    pieces = []
    for c in range(CHUNKS):
        loads[c].wait()
        hi, lo = split2(e_buf[pl.ds(c * chunk, chunk), :])
        two = dot(r_two, hi, 1, 1)
        pieces.append(two[:rank] + two[rank:] + dot(r_hi, lo, 1, 1))
    for i in range(nrow):
        @pl.when(jnp.logical_not(jnp.logical_and(row == col, row == i)))
        def _():
            remote(gr_own, gr_all.at[i], gr_ss.at[0], gr_rs.at[i], {"row": col}).wait_recv()
    gr = gr_all[0]
    for i in range(1, nrow):
        gr = gr + gr_all[i]
    gr_hi, gr_lo = split2(gr)
    two = dot(jnp.concatenate([gr_hi, gr_lo], axis=0), acts[...], 1, 0)
    part_left = jnp.concatenate(pieces, axis=1) + two[:rank] + two[rank:]
    width = rows // nrep
    for k in range(nrep):
        lp[k] = part_left[:, k * width:(k + 1) * width]

    copies = []
    for k in range(1, nrep):
        to = turn(rep, k, nrep)
        cp = remote(lp.at[to], l_rx.at[rep], l_ss.at[k], l_rs.at[k], {"rep": to})
        cp.start()
        copies.append(cp)
    sent += copies
    total = lp[rep]
    for k, cp in enumerate(copies, 1):
        cp.wait_recv()
        total = total + l_rx[turn(rep, nrep - k, nrep)]
    l_own[...] = total
    copies = []
    for k in range(1, nrow):
        cp = remote(l_own, l_row.at[row], lr_ss.at[k], lr_rs.at[k], {"row": turn(row, k, nrow)})
        cp.start()
        copies.append(cp)
    sent += copies
    for cp in bulk[1]:
        cp.start()
    l_row[row] = total
    for cp in copies:
        cp.wait_recv()
    total = l_row[0]
    for i in range(1, nrow):
        total = total + l_row[i]
    lag[rep] = total
    copies = []
    for k in range(1, nrep):
        cp = remote(lag.at[rep], lag.at[rep], la_ss.at[k], la_rs.at[k], {"rep": turn(rep, k, nrep)})
        cp.start()
        copies.append(cp)
    sent += copies
    for cp in copies:
        cp.wait_recv()
    left = jnp.concatenate([lag[k] for k in range(nrep)], axis=1)
    l_hi, l_lo = split2(left)
    l_two = jnp.concatenate([l_hi, l_lo], axis=0)

    gram_all[col] = jnp.zeros(gram_all.shape[1:], F32)
    gram_all[col, :, 0:rank] = dot(left, left, 1, 1, highest)
    gram_copies = []
    for k in range(1, ncol):
        cp = remote(gram_all.at[col], gram_all.at[col], gm_ss.at[k], gm_rs.at[k], {"col": turn(col, k, ncol)})
        cp.start()
        gram_copies.append(cp)
    sent += gram_copies

    own_a.wait()
    own_g.wait()
    for part in bulk:
        for cp in part:
            cp.wait_recv()
    a = a_all[...].reshape(nrow * acts.shape[0], rows)
    g = g_all[...].reshape(ncol * grads.shape[0], cols)
    stores = []
    w = jnp.zeros((rank, cols), F32)
    for c in range(CHUNKS):
        part = pl.ds(c * chunk, chunk)
        t = dot(a[:, c * chunk:(c + 1) * chunk], g, 0, 0) + e_buf[part, :]
        e_buf[part, :] = t
        stores.append(pltpu.make_async_copy(e_buf.at[part], t_out.at[part], tsem.at[c]))
        stores[-1].start()
        hi, lo = split2(t)
        two = dot(l_two[:, c * chunk:(c + 1) * chunk], hi, 1, 0)
        w = w + two[:rank] + two[rank:] + dot(l_hi[:, c * chunk:(c + 1) * chunk], lo, 1, 0)
    lane_tiles = cols // LANES
    tiles = (rank // SUB) * lane_tiles
    for t in range(owners * tpd):
        if t < tiles:
            h, l = divmod(t, lane_tiles)
            w_tx[t // tpd, t % tpd] = w[h * SUB:(h + 1) * SUB, l * LANES:(l + 1) * LANES]
        else:
            w_tx[t // tpd, t % tpd] = jnp.zeros((SUB, LANES), F32)

    copies = []
    for k in range(1, nrep):
        to = turn(rep, k, nrep)
        keep = to < owners
        slot = jnp.minimum(to, owners - 1)
        cp = remote(w_tx.at[slot], w_rx.at[rep], w_ss.at[k], w_rs.at[k], {"rep": to})
        copies.append((cp, keep))

        @pl.when(keep)
        def _():
            cp.start()

    for cp in gram_copies:
        cp.wait_recv()
    gram = gram_all[0]
    for j in range(1, ncol):
        gram = gram + gram_all[j]
    gram = gram[:, 0:rank]
    ri = lax.broadcasted_iota(jnp.int32, (rank, rank), 0)
    ci = lax.broadcasted_iota(jnp.int32, (rank, rank), 1)
    r1 = lax.broadcasted_iota(jnp.int32, (rank, 1), 0)
    inv = jnp.where(ri == ci, 1.0, 0.0).astype(F32)
    for j in range(rank):
        f = jnp.where(r1 > j, gram[:, j:j + 1] / gram[j:j + 1, j:j + 1], 0.0)
        inv = inv - f * inv[j:j + 1, :]
        gram = gram - f * gram[j:j + 1, :]
    diag = jnp.sum(jnp.where(ri == ci, gram, 0.0), axis=1, keepdims=True)
    inv = inv / jnp.sqrt(diag)
    lo_t = dot(inv, left, 1, 0, highest)
    o_hi, o_lo = split2(lo_t)
    los[...] = jnp.concatenate([o_hi, o_hi, o_lo], axis=0)

    mine = rep < owners

    @pl.when(mine)
    def _():
        total = w_tx[jnp.minimum(rep, owners - 1)]
        for k, (cp, keep) in enumerate(copies, 1):
            cp.wait_recv()
            total = total + w_rx[turn(rep, nrep - k, nrep)]
        w_own[...] = total
        ex = []
        for k in range(1, ncol):
            cp = remote(w_own, w_col.at[col], wc_ss.at[k], wc_rs.at[k], {"col": turn(col, k, ncol)})
            cp.start()
            ex.append(cp)
        w_col[col] = total
        for cp in ex:
            cp.wait_recv()
        total = w_col[0]
        for j in range(1, ncol):
            total = total + w_col[j]
        slot = jnp.minimum(rep, owners - 1)
        wag[slot] = total
        for k in range(1, nrep):
            remote(wag.at[slot], wag.at[slot], wa_ss.at[k], wa_rs.at[k], {"rep": turn(rep, k, nrep)}).start()
        for cp in ex:
            cp.wait_send()

    for k in range(1, nrep):
        @pl.when(turn(rep, nrep - k, nrep) < owners)
        def _():
            remote(wag.at[0], wag.at[0], wa_ss.at[k], wa_rs.at[k], {"rep": turn(rep, k, nrep)}).wait_recv()
    halves = []
    for h in range(rank // SUB):
        ts = [h * lane_tiles + l for l in range(lane_tiles)]
        halves.append(jnp.concatenate([wag[t // tpd, t % tpd] for t in ts], axis=1))
    w_all = jnp.concatenate(halves, axis=0)
    nr = dot(inv, w_all, 1, 0, highest) / nrep
    nrt[...] = nr
    n_hi, n_lo = split2(nr)
    nrs[...] = jnp.concatenate([n_hi, n_lo, n_hi], axis=0)

    for cp, is_self in gr_copies:
        @pl.when(jnp.logical_not(is_self))
        def _():
            cp.wait_send()
    for cp in sent:
        cp.wait_send()
    for part in bulk:
        for cp in part:
            cp.wait_send()
    for cp, keep in copies:
        @pl.when(keep)
        def _():
            cp.wait_send()

    @pl.when(mine)
    def _():
        for k in range(1, nrep):
            remote(wag.at[0], wag.at[0], wa_ss.at[k], wa_rs.at[k], {"rep": turn(rep, k, nrep)}).wait_send()
    for cp in stores:
        cp.wait()


def finish_kernel(t, los, nrs, nrt, out, right_out):
    out[...] = t[...] - dot(los[...], nrs[...], 0, 0)

    @pl.when(pl.program_id(0) == 0)
    def _():
        right_out[...] = nrt[...].T


def kernel_body(nrep, nrow, ncol, activations, out_grads, error_buffer, right_factor):
    rows, cols = error_buffer.shape
    rank = right_factor.shape[1]
    ta, tg = activations.shape[0], out_grads.shape[0]
    tiles = (rank // SUB) * (cols // LANES)
    tpd = -(-tiles // nrep)
    owners = -(-tiles // tpd)
    width = rows // nrep
    vmem = pl.BlockSpec(memory_space=pltpu.VMEM)
    hbm = pl.BlockSpec(memory_space=pl.ANY)
    dma = lambda *s: pltpu.SemaphoreType.DMA(s)
    target, los, nrs, nrt = pl.pallas_call(
        functools.partial(factor_kernel, nrep, nrow, ncol, owners, tpd),
        out_shape=(
            jax.ShapeDtypeStruct((rows, cols), F32),
            jax.ShapeDtypeStruct((3 * rank, rows), BF16),
            jax.ShapeDtypeStruct((3 * rank, cols), BF16),
            jax.ShapeDtypeStruct((rank, cols), F32),
        ),
        in_specs=[vmem, vmem, hbm, vmem],
        out_specs=(hbm, vmem, vmem, vmem),
        scratch_shapes=[
            pltpu.VMEM((rows, cols), F32),
            pltpu.VMEM((SUB, LANES), BF16),
            pltpu.VMEM((SUB, LANES), BF16),
            pltpu.VMEM((nrow, ta, rows), BF16),
            pltpu.VMEM((ncol, tg, cols), BF16),
            pltpu.VMEM((rank, tg), F32),
            pltpu.VMEM((nrow, rank, tg), F32),
            pltpu.VMEM((nrep, rank, width), F32),
            pltpu.VMEM((nrep, rank, width), F32),
            pltpu.VMEM((rank, width), F32),
            pltpu.VMEM((nrow, rank, width), F32),
            pltpu.VMEM((nrep, rank, width), F32),
            pltpu.VMEM((ncol, rank, LANES), F32),
            pltpu.VMEM((owners, tpd, SUB, LANES), F32),
            pltpu.VMEM((nrep, tpd, SUB, LANES), F32),
            pltpu.VMEM((tpd, SUB, LANES), F32),
            pltpu.VMEM((ncol, tpd, SUB, LANES), F32),
            pltpu.VMEM((owners, tpd, SUB, LANES), F32),
            dma(CHUNKS), dma(CHUNKS), dma(2),
            dma(2, nrow), dma(2, nrow), dma(2, ncol), dma(2, ncol),
            dma(ncol), dma(nrow),
            dma(nrep), dma(nrep), dma(nrow), dma(nrow), dma(nrep), dma(nrep), dma(ncol), dma(ncol),
            dma(nrep), dma(nrep), dma(ncol), dma(ncol), dma(nrep), dma(nrep),
        ],
        compiler_params=pltpu.CompilerParams(collective_id=0, has_side_effects=True),
        name="factors",
    )(activations, out_grads, error_buffer, right_factor)
    steps = 8
    block = rows // steps
    return pl.pallas_call(
        finish_kernel,
        grid=(steps,),
        out_shape=(
            jax.ShapeDtypeStruct((rows, cols), F32),
            jax.ShapeDtypeStruct((cols, rank), F32),
        ),
        in_specs=[
            pl.BlockSpec((block, cols), lambda i: (i, 0)),
            pl.BlockSpec((3 * rank, block), lambda i: (0, i)),
            pl.BlockSpec((3 * rank, cols), lambda i: (0, 0)),
            pl.BlockSpec((rank, cols), lambda i: (0, 0)),
        ],
        out_specs=(
            pl.BlockSpec((block, cols), lambda i: (i, 0)),
            pl.BlockSpec((cols, rank), lambda i: (0, 0)),
        ),
        name="finish",
    )(target, los, nrs, nrt)


def body(activations, out_grads, error_buffer, right_factor):
    nrep, nrow, ncol = (lax.axis_size(a) for a in ("rep", "row", "col"))
    rows, cols = error_buffer.shape
    rank = right_factor.shape[1]
    fits = (
        nrep <= 16
        and nrow == ncol
        and activations.shape[0] % LANES == 0
        and rows % (nrep * LANES) == 0
        and rows % (8 * LANES) == 0
        and cols % LANES == 0
        and rank % 16 == 0
        and rank <= LANES
        and rows * cols * 4 <= 2**23
    )
    if not fits:
        return plain_body(activations, out_grads, error_buffer, right_factor)
    return kernel_body(nrep, nrow, ncol, activations, out_grads, error_buffer, right_factor)


def solution(mesh):
    return jax.shard_map(
        body,
        mesh=mesh,
        in_specs=(
            P(("rep", "row"), "col"),
            P(("rep", "col"), "row"),
            P(("rep", "col"), "row"),
            P("row", None),
        ),
        out_specs=(P(("rep", "col"), "row"), P("row", None)),
        check_vma=False,
    )
```

time: 201 us -> 48.4 us (0.24)
  blocking collectives: 86.8 us -> 0 us
  waiting for transfers between devices: 67.1 us -> 0 us
  Pallas kernels: 0 us -> 43.5 us
  matrix products: 25.6 us -> 0 us
  between operations: 14.1 us -> 0.64 us
  other arithmetic: 4.02 us -> 0 us
    all_gather x4 -> x0, blocking collectives: 44.4 us -> none  [the longest x1 16.9 us: body(): gathered_acts = lax.all_gather(activations, 'row', axis=0, tiled=True)]
    pallas_call x0 -> x2, Pallas kernels: none -> 43.5 us  [the longest x1 35.3 us: kernel_body(): pl.pallas_call(functools.partial(factor_kernel, nrep, nrow, ncol, owners,...]
    psum x3 -> x0, blocking collectives: 42.4 us -> none  [the longest x1 28.3 us: body(): lax.psum(jnp.dot(left_part.T, left_part, precision=highest), ('rep', 'col'))]
    unnamed x3 -> x0, waiting for transfers between devices: 33.7 us -> none
    reduce_scatter x1 -> x0, waiting for transfers between devices: 33.4 us -> none  [body(): lax.psum_scatter(jnp.dot(block, right_factor, precision=highest), 'rep',...]
    dot_general x4 -> x0, matrix products: 15.3 us -> none  [the longest x1 7.23 us: body(): approx = jnp.dot(left_orth, new_right.T, precision=highest)]
    unnamed x1 -> x0, matrix products: 10.2 us -> none
    another operation x5 -> x0, other arithmetic: 4.01 us -> none  [the longest x3 2.13 us: body(): lower = jnp.linalg.cholesky(gram)]
  transfers between devices with their start and end apart: 2 -> 0, of which waited for: 2 -> 0; matrix products, arithmetic and copies ran while one was open for 0% -> 0% of each run, Pallas kernels for 0% -> 0%
where the time goes in v1:
time: 48.4 us; the launch traced here: 48 us
  Pallas kernels  43.5 us (90%)
  local copies, waits for them, and re-layouts  3.84 us (8%)
  between operations  0.64 us (1%)
    pallas_call x1, Pallas kernels, kernel_body(): pl.pallas_call(functools.partial(factor_kernel, nrep, nrow, ncol, owners,...  35.3 us
    pallas_call x1, Pallas kernels, kernel_body(): pl.pallas_call(finish_kernel, grid=(steps,), out_shape=(jax.ShapeDtypeStr...  8.19 us
    unnamed x1, local copies, waits for them, and re-layouts  1.94 us
    pallas_call x1, local copies, waits for them, and re-layouts, kernel_body(): pl.pallas_call(finish_kernel, grid=(steps,), out_shape=(jax.ShapeDtypeStr...  1.9 us

profile of v1, /device:TPU:0, one launch (start us, length us, event | category | flops | bytes accessed | tf_op | source)
XLA Modules:
  0.0 48.0 jit_solution(1262630996362369272)
XLA Ops:
  0.6 1.9 %copy.6.right = f32[1152,16]{1,0:T(8,128)} copy(f32[1152,16]{0,1:T(8,128)} %param.7) | data formatting | bytes 147456 | tf_op args[3]
  2.6 35.3 %factors.1 = (f32[1024,1152]{1,0:T(8,128)}, bf16[48,1024]{1,0:T(8,128)(2,1)}, bf16[48,1152]{1,0:T(8,128)(2,1)}, f32[16,1152]{1,0:T(8,128)}) custom-call(bf16[128,1024]{1,0:T(8,128)(2,1)} %acts.1, bf16[128,1152]{1,0:T(8,128)(2,1)} %grads.1, f32[1024,1152]{1,0:T(8,128)} %err.1, f32[1152,16]{1,0:T(8,128)} %copy.6.right), custom_call_target="tpu_custom_call" | custom-call | tf_op jit(solution)/shard_map/factors/pallas_call | solution.py:351
  37.9 8.2 %finish.1 = (f32[1024,1152]{1,0:T(8,128)}, f32[1152,16]{1,0:T(8,128)}) custom-call(f32[1024,1152]{1,0:T(8,128)} %get-tuple-element.6.t, bf16[48,1024]{1,0:T(8,128)(2,1)} %get-tuple-element.7.los, bf16[48,1152]{1,0:T(8,128)(2,1)} %get-tuple-element.8.nrs, f32[16,1152]{1,0:T(8,128)} %get-tuple-element.9.nrt), custom_call_target="tpu_custom_call" | custom-call | tf_op jit(solution)/shard_map/finish/pallas_call | solution.py:391
  46.1 1.9 %copy.7 = f32[1152,16]{0,1:T(8,128)} copy(f32[1152,16]{1,0:T(8,128)} %get-tuple-element.11) | data formatting | bytes 147456 | tf_op jit(solution)/shard_map/finish/pallas_call | solution.py:391

commit v2 on v1

--- a/solution.py
+++ b/solution.py
@@ -13,6 +13,8 @@
 LANES = 128
 SUB = 8
 CHUNKS = 4
+QUARTERS = 4
+GRANT = 24 * 2**20
 
 
 def plain_body(activations, out_grads, error_buffer, right_factor):
@@ -58,17 +60,17 @@
 
 def factor_kernel(
     nrep, nrow, ncol, owners, tpd,
-    acts, grads, err, right,
-    t_out, los, nrs, nrt,
-    e_buf, t_hi, t_lo, a_all, g_all, gr_own, gr_all,
+    acts_in, grads_in, err, right_in,
+    target, los, nrs, nrt,
+    e_hi, e_lo, right_t, a_all, g_all, gr_own, gr_all, la_own, la_all,
     lp, l_rx, l_own, l_row, lag, gram_all, w_tx, w_rx, w_own, w_col, wag,
-    esem, tsem, loc_sem, a_ss, a_rs, g_ss, g_rs, gr_ss, gr_rs,
+    esem, loc_sem, a_ss, a_rs, g_ss, g_rs, gr_ss, gr_rs, lt_ss, lt_rs,
     l_ss, l_rs, lr_ss, lr_rs, la_ss, la_rs, gm_ss, gm_rs,
     w_ss, w_rs, wc_ss, wc_rs, wa_ss, wa_rs,
 ):
     rep, row, col = lax.axis_index("rep"), lax.axis_index("row"), lax.axis_index("col")
-    rows, cols = e_buf.shape
-    rank = right.shape[1]
+    rows, cols = target.shape
+    rank = right_t.shape[0]
     chunk = rows // CHUNKS
     highest = lax.Precision.HIGHEST
     sent = []
@@ -82,8 +84,6 @@
         return lax.rem(i + k, n)
 
     barrier = pltpu.get_barrier_semaphore()
-    for k in range(1, nrep):
-        pl.semaphore_signal(barrier, inc=1, device_id={"rep": turn(rep, k, nrep)}, device_id_type=MESH)
     for i in range(nrow):
         for j in range(ncol):
             if i or j:
@@ -92,22 +92,43 @@
                     device_id={"row": turn(row, i, nrow), "col": turn(col, j, ncol)},
                     device_id_type=MESH,
                 )
-
+    for k in range(1, nrep):
+        pl.semaphore_signal(barrier, inc=1, device_id={"rep": turn(rep, k, nrep)}, device_id_type=MESH)
+
+    acts, grads = a_all.at[row], g_all.at[col]
+    own_r = pltpu.make_async_copy(right_in, right_t, loc_sem.at[0])
+    own_g = pltpu.make_async_copy(grads_in, grads, loc_sem.at[1])
+    own_a = pltpu.make_async_copy(acts_in, acts, loc_sem.at[2])
+    own_r.start()
+    own_g.start()
     loads = []
     for c in range(CHUNKS):
         part = pl.ds(c * chunk, chunk)
-        loads.append(pltpu.make_async_copy(err.at[part], e_buf.at[part], esem.at[c]))
+        loads.append(pltpu.make_async_copy(err.at[part], target.at[part], esem.at[c]))
         loads[-1].start()
-    own_a = pltpu.make_async_copy(acts, a_all.at[row], loc_sem.at[0])
-    own_g = pltpu.make_async_copy(grads, g_all.at[col], loc_sem.at[1])
     own_a.start()
-    own_g.start()
-
-    right_t = right[...].T
-    r_hi, r_lo = split2(right_t)
+    own_r.wait()
+    own_g.wait()
+    r_hi, r_lo = split2(right_t[...])
     r_two = jnp.concatenate([r_hi, r_lo], axis=0)
     gr2 = dot(r_two, grads[...], 1, 1)
     gr_own[...] = gr2[:rank] + gr2[rank:]
+
+    pieces = []
+
+    def error_term(c):
+        loads[c].wait()
+        part = pl.ds(c * chunk, chunk)
+        hi, lo = split2(target[part, :])
+        e_hi[part, :] = hi
+        e_lo[part, :] = lo
+        two = dot(r_two, hi, 1, 1)
+        pieces.append(two[:rank] + two[rank:] + dot(r_hi, lo, 1, 1))
+
+    early = CHUNKS // 2
+    for c in range(early):
+        error_term(c)
+    own_a.wait()
 
     pl.semaphore_wait(barrier, nrep - 1 + nrow * ncol - 1)
 
@@ -125,26 +146,21 @@
     def _():
         gr_all[row] = gr_own[...]
 
-    ta, tg = acts.shape[0] // 2, grads.shape[0] // 2
+    ta, tg = acts.shape[0] // QUARTERS, grads.shape[0] // QUARTERS
     bulk = []
-    for half in range(2):
-        part = []
+    for q in range(QUARTERS):
         for k in range(1, nrow):
-            s = pl.ds(half * ta, ta)
-            part.append(remote(acts.at[s], a_all.at[row, s], a_ss.at[half, k], a_rs.at[half, k], {"row": turn(row, k, nrow)}))
+            s = pl.ds(q * ta, ta)
+            bulk.append(remote(a_all.at[row, s], a_all.at[row, s], a_ss.at[q, k], a_rs.at[q, k], {"row": turn(row, k, nrow)}))
         for k in range(1, ncol):
-            s = pl.ds(half * tg, tg)
-            part.append(remote(grads.at[s], g_all.at[col, s], g_ss.at[half, k], g_rs.at[half, k], {"col": turn(col, k, ncol)}))
-        bulk.append(part)
-    for cp in bulk[0]:
-        cp.start()
-
-    pieces = []
-    for c in range(CHUNKS):
-        loads[c].wait()
-        hi, lo = split2(e_buf[pl.ds(c * chunk, chunk), :])
-        two = dot(r_two, hi, 1, 1)
-        pieces.append(two[:rank] + two[rank:] + dot(r_hi, lo, 1, 1))
+            s = pl.ds(q * tg, tg)
+            bulk.append(remote(g_all.at[col, s], g_all.at[col, s], g_ss.at[q, k], g_rs.at[q, k], {"col": turn(col, k, ncol)}))
+    per = nrow + ncol - 2
+    for cp in bulk[:2 * per]:
+        cp.start()
+
+    for c in range(early, CHUNKS):
+        error_term(c)
     for i in range(nrow):
         @pl.when(jnp.logical_not(jnp.logical_and(row == col, row == i)))
         def _():
@@ -177,7 +193,7 @@
         cp.start()
         copies.append(cp)
     sent += copies
-    for cp in bulk[1]:
+    for cp in bulk[2 * per:3 * per]:
         cp.start()
     l_row[row] = total
     for cp in copies:
@@ -198,6 +214,22 @@
     l_hi, l_lo = split2(left)
     l_two = jnp.concatenate([l_hi, l_lo], axis=0)
 
+    la2 = dot(l_two, acts[...], 1, 1)
+    la_own[...] = la2[:rank] + la2[rank:]
+    lt_copies = []
+    for i in range(nrow):
+        cp = remote(la_own, la_all.at[col], lt_ss.at[i], lt_rs.at[col], {"row": i, "col": row})
+        is_self = jnp.logical_and(row == col, row == i)
+        lt_copies.append((cp, is_self))
+
+        @pl.when(jnp.logical_not(is_self))
+        def _():
+            cp.start()
+
+    @pl.when(row == col)
+    def _():
+        la_all[col] = la_own[...]
+
     gram_all[col] = jnp.zeros(gram_all.shape[1:], F32)
     gram_all[col, :, 0:rank] = dot(left, left, 1, 1, highest)
     gram_copies = []
@@ -206,25 +238,21 @@
         cp.start()
         gram_copies.append(cp)
     sent += gram_copies
-
-    own_a.wait()
-    own_g.wait()
-    for part in bulk:
-        for cp in part:
-            cp.wait_recv()
-    a = a_all[...].reshape(nrow * acts.shape[0], rows)
-    g = g_all[...].reshape(ncol * grads.shape[0], cols)
-    stores = []
-    w = jnp.zeros((rank, cols), F32)
-    for c in range(CHUNKS):
-        part = pl.ds(c * chunk, chunk)
-        t = dot(a[:, c * chunk:(c + 1) * chunk], g, 0, 0) + e_buf[part, :]
-        e_buf[part, :] = t
-        stores.append(pltpu.make_async_copy(e_buf.at[part], t_out.at[part], tsem.at[c]))
-        stores[-1].start()
-        hi, lo = split2(t)
-        two = dot(l_two[:, c * chunk:(c + 1) * chunk], hi, 1, 0)
-        w = w + two[:rank] + two[rank:] + dot(l_hi[:, c * chunk:(c + 1) * chunk], lo, 1, 0)
+    for cp in bulk[3 * per:]:
+        cp.start()
+
+    two = dot(l_two, e_hi[...], 1, 0)
+    w = two[:rank] + two[rank:] + dot(l_hi, e_lo[...], 1, 0)
+    for j in range(ncol):
+        @pl.when(jnp.logical_not(jnp.logical_and(row == col, col == j)))
+        def _():
+            remote(la_own, la_all.at[j], lt_ss.at[0], lt_rs.at[j], {"col": row}).wait_recv()
+    la = la_all[0]
+    for j in range(1, ncol):
+        la = la + la_all[j]
+    la_hi, la_lo = split2(la)
+    two = dot(jnp.concatenate([la_hi, la_lo], axis=0), grads[...], 1, 0)
+    w = w + two[:rank] + two[rank:]
     lane_tiles = cols // LANES
     tiles = (rank // SUB) * lane_tiles
     for t in range(owners * tpd):
@@ -262,41 +290,62 @@
         gram = gram - f * gram[j:j + 1, :]
     diag = jnp.sum(jnp.where(ri == ci, gram, 0.0), axis=1, keepdims=True)
     inv = inv / jnp.sqrt(diag)
-    lo_t = dot(inv, left, 1, 0, highest)
-    o_hi, o_lo = split2(lo_t)
-    los[...] = jnp.concatenate([o_hi, o_hi, o_lo], axis=0)
 
     mine = rep < owners
+    own_slot = jnp.minimum(rep, owners - 1)
+    ex = [
+        remote(w_own, w_col.at[col], wc_ss.at[k], wc_rs.at[k], {"col": turn(col, k, ncol)})
+        for k in range(1, ncol)
+    ]
+    gather = [
+        remote(wag.at[own_slot], wag.at[own_slot], wa_ss.at[k], wa_rs.at[k], {"rep": turn(rep, k, nrep)})
+        for k in range(1, nrep)
+    ]
 
     @pl.when(mine)
     def _():
-        total = w_tx[jnp.minimum(rep, owners - 1)]
+        total = w_tx[own_slot]
         for k, (cp, keep) in enumerate(copies, 1):
             cp.wait_recv()
             total = total + w_rx[turn(rep, nrep - k, nrep)]
         w_own[...] = total
-        ex = []
-        for k in range(1, ncol):
-            cp = remote(w_own, w_col.at[col], wc_ss.at[k], wc_rs.at[k], {"col": turn(col, k, ncol)})
+        w_col[col] = total
+        for cp in ex:
             cp.start()
-            ex.append(cp)
-        w_col[col] = total
+
+    for cp in bulk:
+        cp.wait_recv()
+
+    def target_term(c):
+        part = pl.ds(c * chunk, chunk)
+        a = a_all[:, :, c * chunk:(c + 1) * chunk].reshape(nrow * acts.shape[0], chunk)
+        g = g_all[...].reshape(ncol * grads.shape[0], cols)
+        target[part, :] = dot(a, g, 0, 0) + target[part, :]
+
+    for c in range(early):
+        target_term(c)
+
+    @pl.when(mine)
+    def _():
         for cp in ex:
             cp.wait_recv()
         total = w_col[0]
         for j in range(1, ncol):
             total = total + w_col[j]
-        slot = jnp.minimum(rep, owners - 1)
-        wag[slot] = total
-        for k in range(1, nrep):
-            remote(wag.at[slot], wag.at[slot], wa_ss.at[k], wa_rs.at[k], {"rep": turn(rep, k, nrep)}).start()
-        for cp in ex:
-            cp.wait_send()
+        wag[own_slot] = total
+        for cp in gather:
+            cp.start()
+
+    lo_t = dot(inv, left, 1, 0, highest)
+    o_hi, o_lo = split2(lo_t)
+    los[...] = jnp.concatenate([o_hi, o_hi, o_lo], axis=0)
+    for c in range(early, CHUNKS):
+        target_term(c)
 
     for k in range(1, nrep):
         @pl.when(turn(rep, nrep - k, nrep) < owners)
         def _():
-            remote(wag.at[0], wag.at[0], wa_ss.at[k], wa_rs.at[k], {"rep": turn(rep, k, nrep)}).wait_recv()
+            gather[k - 1].wait_recv()
     halves = []
     for h in range(rank // SUB):
         ts = [h * lane_tiles + l for l in range(lane_tiles)]
@@ -307,15 +356,12 @@
     n_hi, n_lo = split2(nr)
     nrs[...] = jnp.concatenate([n_hi, n_lo, n_hi], axis=0)
 
-    for cp, is_self in gr_copies:
+    for cp, is_self in gr_copies + lt_copies:
         @pl.when(jnp.logical_not(is_self))
         def _():
             cp.wait_send()
-    for cp in sent:
+    for cp in sent + bulk:
         cp.wait_send()
-    for part in bulk:
-        for cp in part:
-            cp.wait_send()
     for cp, keep in copies:
         @pl.when(keep)
         def _():
@@ -323,18 +369,23 @@
 
     @pl.when(mine)
     def _():
-        for k in range(1, nrep):
-            remote(wag.at[0], wag.at[0], wa_ss.at[k], wa_rs.at[k], {"rep": turn(rep, k, nrep)}).wait_send()
+        for cp in ex + gather:
+            cp.wait_send()
+
+
+def finish_kernel(t, los, nrs, nrt, out, right_out, buf, sem):
+    rows = t.shape[0]
+    steps = sem.shape[0]
+    block = rows // steps
+    stores = []
+    for c in range(steps):
+        part = pl.ds(c * block, block)
+        buf[part, :] = t[part, :] - dot(los[:, c * block:(c + 1) * block], nrs[...], 0, 0)
+        stores.append(pltpu.make_async_copy(buf.at[part], out.at[part], sem.at[c]))
+        stores[-1].start()
+    right_out[...] = nrt[...]
     for cp in stores:
         cp.wait()
-
-
-def finish_kernel(t, los, nrs, nrt, out, right_out):
-    out[...] = t[...] - dot(los[...], nrs[...], 0, 0)
-
-    @pl.when(pl.program_id(0) == 0)
-    def _():
-        right_out[...] = nrt[...].T
 
 
 def kernel_body(nrep, nrow, ncol, activations, out_grads, error_buffer, right_factor):
@@ -346,26 +397,28 @@
     owners = -(-tiles // tpd)
     width = rows // nrep
     vmem = pl.BlockSpec(memory_space=pltpu.VMEM)
-    hbm = pl.BlockSpec(memory_space=pl.ANY)
+    hbm = pl.BlockSpec(memory_space=pltpu.HBM)
     dma = lambda *s: pltpu.SemaphoreType.DMA(s)
     target, los, nrs, nrt = pl.pallas_call(
         functools.partial(factor_kernel, nrep, nrow, ncol, owners, tpd),
         out_shape=(
-            jax.ShapeDtypeStruct((rows, cols), F32),
-            jax.ShapeDtypeStruct((3 * rank, rows), BF16),
-            jax.ShapeDtypeStruct((3 * rank, cols), BF16),
-            jax.ShapeDtypeStruct((rank, cols), F32),
+            pltpu.VMEM((rows, cols), F32),
+            pltpu.VMEM((3 * rank, rows), BF16),
+            pltpu.VMEM((3 * rank, cols), BF16),
+            pltpu.VMEM((rank, cols), F32),
         ),
-        in_specs=[vmem, vmem, hbm, vmem],
-        out_specs=(hbm, vmem, vmem, vmem),
+        in_specs=[hbm] * 4,
+        out_specs=(vmem, vmem, vmem, vmem),
         scratch_shapes=[
-            pltpu.VMEM((rows, cols), F32),
-            pltpu.VMEM((SUB, LANES), BF16),
-            pltpu.VMEM((SUB, LANES), BF16),
+            pltpu.VMEM((rows, cols), BF16),
+            pltpu.VMEM((rows, cols), BF16),
+            pltpu.VMEM((rank, cols), F32),
             pltpu.VMEM((nrow, ta, rows), BF16),
             pltpu.VMEM((ncol, tg, cols), BF16),
             pltpu.VMEM((rank, tg), F32),
             pltpu.VMEM((nrow, rank, tg), F32),
+            pltpu.VMEM((rank, ta), F32),
+            pltpu.VMEM((ncol, rank, ta), F32),
             pltpu.VMEM((nrep, rank, width), F32),
             pltpu.VMEM((nrep, rank, width), F32),
             pltpu.VMEM((rank, width), F32),
@@ -377,36 +430,31 @@
             pltpu.VMEM((tpd, SUB, LANES), F32),
             pltpu.VMEM((ncol, tpd, SUB, LANES), F32),
             pltpu.VMEM((owners, tpd, SUB, LANES), F32),
-            dma(CHUNKS), dma(CHUNKS), dma(2),
-            dma(2, nrow), dma(2, nrow), dma(2, ncol), dma(2, ncol),
-            dma(ncol), dma(nrow),
+            dma(CHUNKS), dma(3),
+            dma(QUARTERS, nrow), dma(QUARTERS, nrow), dma(QUARTERS, ncol), dma(QUARTERS, ncol),
+            dma(ncol), dma(nrow), dma(nrow), dma(ncol),
             dma(nrep), dma(nrep), dma(nrow), dma(nrow), dma(nrep), dma(nrep), dma(ncol), dma(ncol),
             dma(nrep), dma(nrep), dma(ncol), dma(ncol), dma(nrep), dma(nrep),
         ],
-        compiler_params=pltpu.CompilerParams(collective_id=0, has_side_effects=True),
+        compiler_params=pltpu.CompilerParams(
+            collective_id=0, has_side_effects=True, vmem_limit_bytes=GRANT
+        ),
         name="factors",
-    )(activations, out_grads, error_buffer, right_factor)
+    )(activations, out_grads, error_buffer, right_factor.T)
     steps = 8
-    block = rows // steps
-    return pl.pallas_call(
+    new_error, new_right = pl.pallas_call(
         finish_kernel,
-        grid=(steps,),
         out_shape=(
             jax.ShapeDtypeStruct((rows, cols), F32),
-            jax.ShapeDtypeStruct((cols, rank), F32),
+            jax.ShapeDtypeStruct((rank, cols), F32),
         ),
-        in_specs=[
-            pl.BlockSpec((block, cols), lambda i: (i, 0)),
-            pl.BlockSpec((3 * rank, block), lambda i: (0, i)),
-            pl.BlockSpec((3 * rank, cols), lambda i: (0, 0)),
-            pl.BlockSpec((rank, cols), lambda i: (0, 0)),
-        ],
-        out_specs=(
-            pl.BlockSpec((block, cols), lambda i: (i, 0)),
-            pl.BlockSpec((cols, rank), lambda i: (0, 0)),
-        ),
+        in_specs=[vmem, vmem, vmem, vmem],
+        out_specs=(hbm, vmem),
+        scratch_shapes=[pltpu.VMEM((rows, cols), F32), dma(steps)],
+        compiler_params=pltpu.CompilerParams(vmem_limit_bytes=GRANT),
         name="finish",
     )(target, los, nrs, nrt)
+    return new_error, new_right.T
 
 
 def body(activations, out_grads, error_buffer, right_factor):

time: 48.4 us -> 42.6 us (0.88)
  Pallas kernels: 43.5 us -> 36.6 us
  local copies, waits for them, and re-layouts: 3.84 us -> 5.12 us
    pallas_call x1, Pallas kernels: 8.19 us -> 3.15 us  [kernel_body(): pl.pallas_call(finish_kernel, out_shape=(jax.ShapeDtypeStruct((rows, cols...]
    unnamed x1 -> x8, local copies, waits for them, and re-layouts: 1.94 us -> 5.12 us
    pallas_call x1 -> x0, local copies, waits for them, and re-layouts: 1.9 us -> none  [kernel_body(): pl.pallas_call(finish_kernel, grid=(steps,), out_shape=(jax.ShapeDtypeStr...]
    pallas_call x1, Pallas kernels: 35.3 us -> 33.4 us  [kernel_body(): pl.pallas_call(functools.partial(factor_kernel, nrep, nrow, ncol, owners,...]
where the time goes in v2:
time: 42.6 us; the launch traced here: 42.4 us
  Pallas kernels  36.6 us (86%)
  local copies, waits for them, and re-layouts  5.12 us (12%)
  between operations  0.65 us (2%)
    pallas_call x1, Pallas kernels, kernel_body(): pl.pallas_call(functools.partial(factor_kernel, nrep, nrow, ncol, owners,...  33.4 us
    unnamed x8, local copies, waits for them, and re-layouts  5.12 us
    pallas_call x1, Pallas kernels, kernel_body(): pl.pallas_call(finish_kernel, out_shape=(jax.ShapeDtypeStruct((rows, cols...  3.15 us

profile of v2, /device:TPU:0, one launch (start us, length us, event | category | flops | bytes accessed | tf_op | source)
XLA Modules:
  0.0 42.4 jit_solution(14161229372185191015)
XLA Ops:
  0.6 0.0 copy-start
  0.6 2.3 %copy-done = f32[1024,1152]{1,0:T(8,128)S(1)} copy-done((f32[1024,1152]{1,0:T(8,128)S(1)}, f32[1024,1152]{1,0:T(8,128)}, u32[]{:S(2)}) %copy-start) | copy-done | bytes 4718616
  3.0 0.0 copy-start.1
  3.0 1.0 %copy-done.1 = bf16[128,1152]{1,0:T(8,128)(2,1)S(1)} copy-done((bf16[128,1152]{1,0:T(8,128)(2,1)S(1)}, bf16[128,1152]{1,0:T(8,128)(2,1)}, u32[]{:S(2)}) %copy-start.1) | copy-done | bytes 294936
  3.9 0.0 copy-start.2
  3.9 0.9 %copy-done.2 = bf16[128,1024]{1,0:T(8,128)(2,1)S(1)} copy-done((bf16[128,1024]{1,0:T(8,128)(2,1)S(1)}, bf16[128,1024]{1,0:T(8,128)(2,1)}, u32[]{:S(2)}) %copy-start.2) | copy-done | bytes 262168
  4.9 0.0 copy-start.3
  4.9 0.9 %copy-done.3 = f32[1152,16]{0,1:T(8,128)S(1)} copy-done((f32[1152,16]{0,1:T(8,128)S(1)}, f32[1152,16]{0,1:T(8,128)}, u32[]{:S(2)}) %copy-start.3) | copy-done | bytes 73752
  5.8 33.4 %factors.1 = (f32[1024,1152]{1,0:T(8,128)S(1)}, bf16[48,1024]{1,0:T(8,128)(2,1)S(1)}, bf16[48,1152]{1,0:T(8,128)(2,1)S(1)}, f32[16,1152]{1,0:T(8,128)S(1)}) custom-call(bf16[128,1024]{1,0:T(8,128)(2,1)S(1)} %copy-done.2, bf16[128,1152]{1,0:T(8,128)(2,1)S(1)} %copy-done.1, f32[1024,1152]{1,0:T(8,128)S(1)} %copy-done, f32[16,1152]{1,0:T(8,128)S(1)} %bitcast.2), custom_call_target="tpu_custom_call" | custom-call | tf_op jit(solution)/shard_map/factors/pallas_call | solution.py:402
  39.2 3.1 %finish.1 = (f32[1024,1152]{1,0:T(8,128)}, f32[16,1152]{1,0:T(8,128)}) custom-call(f32[1024,1152]{1,0:T(8,128)S(1)} %get-tuple-element.8.t, bf16[48,1024]{1,0:T(8,128)(2,1)S(1)} %get-tuple-element.9.los, bf16[48,1152]{1,0:T(8,128)(2,1)S(1)} %get-tuple-element.10.nrs, f32[16,1152]{1,0:T(8,128)S(1)} %get-tuple-element.11.nrt), custom_call_target="tpu_custom_call" | custom-call | tf_op jit(solution)/shard_map/finish/pallas_call | solution.py:445
Async XLA Ops:
  0.6 2.3 %copy-start = (f32[1024,1152]{1,0:T(8,128)S(1)}, f32[1024,1152]{1,0:T(8,128)}, u32[]{:S(2)}) copy-start(f32[1024,1152]{1,0:T(8,128)} %err.1) | copy-start | bytes 14155780
  3.0 1.0 %copy-start.1 = (bf16[128,1152]{1,0:T(8,128)(2,1)S(1)}, bf16[128,1152]{1,0:T(8,128)(2,1)}, u32[]{:S(2)}) copy-start(bf16[128,1152]{1,0:T(8,128)(2,1)} %grads_in.1) | copy-start | bytes 884740
  3.9 0.9 %copy-start.2 = (bf16[128,1024]{1,0:T(8,128)(2,1)S(1)}, bf16[128,1024]{1,0:T(8,128)(2,1)}, u32[]{:S(2)}) copy-start(bf16[128,1024]{1,0:T(8,128)(2,1)} %acts_in.1) | copy-start | bytes 786436
  4.9 0.9 %copy-start.3 = (f32[1152,16]{0,1:T(8,128)S(1)}, f32[1152,16]{0,1:T(8,128)}, u32[]{:S(2)}) copy-start(f32[1152,16]{0,1:T(8,128)} %param.7) | copy-start | bytes 221188

commit v3 on v2

--- a/solution.py
+++ b/solution.py
@@ -62,9 +62,9 @@
     nrep, nrow, ncol, owners, tpd,
     acts_in, grads_in, err, right_in,
     target, los, nrs, nrt,
-    e_hi, e_lo, right_t, a_all, g_all, gr_own, gr_all, la_own, la_all,
+    e_hi, e_lo, right_t, a_all, g_all, gr_own, gr_all,
     lp, l_rx, l_own, l_row, lag, gram_all, w_tx, w_rx, w_own, w_col, wag,
-    esem, loc_sem, a_ss, a_rs, g_ss, g_rs, gr_ss, gr_rs, lt_ss, lt_rs,
+    esem, loc_sem, a_ss, a_rs, g_ss, g_rs, gr_ss, gr_rs,
     l_ss, l_rs, lr_ss, lr_rs, la_ss, la_rs, gm_ss, gm_rs,
     w_ss, w_rs, wc_ss, wc_rs, wa_ss, wa_rs,
 ):
@@ -193,7 +193,7 @@
         cp.start()
         copies.append(cp)
     sent += copies
-    for cp in bulk[2 * per:3 * per]:
+    for cp in bulk[2 * per:]:
         cp.start()
     l_row[row] = total
     for cp in copies:
@@ -214,22 +214,6 @@
     l_hi, l_lo = split2(left)
     l_two = jnp.concatenate([l_hi, l_lo], axis=0)
 
-    la2 = dot(l_two, acts[...], 1, 1)
-    la_own[...] = la2[:rank] + la2[rank:]
-    lt_copies = []
-    for i in range(nrow):
-        cp = remote(la_own, la_all.at[col], lt_ss.at[i], lt_rs.at[col], {"row": i, "col": row})
-        is_self = jnp.logical_and(row == col, row == i)
-        lt_copies.append((cp, is_self))
-
-        @pl.when(jnp.logical_not(is_self))
-        def _():
-            cp.start()
-
-    @pl.when(row == col)
-    def _():
-        la_all[col] = la_own[...]
-
     gram_all[col] = jnp.zeros(gram_all.shape[1:], F32)
     gram_all[col, :, 0:rank] = dot(left, left, 1, 1, highest)
     gram_copies = []
@@ -238,20 +222,16 @@
         cp.start()
         gram_copies.append(cp)
     sent += gram_copies
-    for cp in bulk[3 * per:]:
-        cp.start()
 
     two = dot(l_two, e_hi[...], 1, 0)
     w = two[:rank] + two[rank:] + dot(l_hi, e_lo[...], 1, 0)
-    for j in range(ncol):
-        @pl.when(jnp.logical_not(jnp.logical_and(row == col, col == j)))
-        def _():
-            remote(la_own, la_all.at[j], lt_ss.at[0], lt_rs.at[j], {"col": row}).wait_recv()
-    la = la_all[0]
-    for j in range(1, ncol):
-        la = la + la_all[j]
-    la_hi, la_lo = split2(la)
-    two = dot(jnp.concatenate([la_hi, la_lo], axis=0), grads[...], 1, 0)
+    for cp in bulk:
+        cp.wait_recv()
+    a_full = a_all[...].reshape(nrow * acts_in.shape[0], rows)
+    g_full = g_all[...].reshape(ncol * grads_in.shape[0], cols)
+    la2 = dot(l_two, a_full, 1, 1)
+    la_hi, la_lo = split2(la2[:rank] + la2[rank:])
+    two = dot(jnp.concatenate([la_hi, la_lo], axis=0), g_full, 1, 0)
     w = w + two[:rank] + two[rank:]
     lane_tiles = cols // LANES
     tiles = (rank // SUB) * lane_tiles
@@ -313,9 +293,6 @@
         for cp in ex:
             cp.start()
 
-    for cp in bulk:
-        cp.wait_recv()
-
     def target_term(c):
         part = pl.ds(c * chunk, chunk)
         a = a_all[:, :, c * chunk:(c + 1) * chunk].reshape(nrow * acts.shape[0], chunk)
@@ -356,7 +333,7 @@
     n_hi, n_lo = split2(nr)
     nrs[...] = jnp.concatenate([n_hi, n_lo, n_hi], axis=0)
 
-    for cp, is_self in gr_copies + lt_copies:
+    for cp, is_self in gr_copies:
         @pl.when(jnp.logical_not(is_self))
         def _():
             cp.wait_send()
@@ -417,8 +394,6 @@
             pltpu.VMEM((ncol, tg, cols), BF16),
             pltpu.VMEM((rank, tg), F32),
             pltpu.VMEM((nrow, rank, tg), F32),
-            pltpu.VMEM((rank, ta), F32),
-            pltpu.VMEM((ncol, rank, ta), F32),
             pltpu.VMEM((nrep, rank, width), F32),
             pltpu.VMEM((nrep, rank, width), F32),
             pltpu.VMEM((rank, width), F32),
@@ -432,7 +407,7 @@
             pltpu.VMEM((owners, tpd, SUB, LANES), F32),
             dma(CHUNKS), dma(3),
             dma(QUARTERS, nrow), dma(QUARTERS, nrow), dma(QUARTERS, ncol), dma(QUARTERS, ncol),
-            dma(ncol), dma(nrow), dma(nrow), dma(ncol),
+            dma(ncol), dma(nrow),
             dma(nrep), dma(nrep), dma(nrow), dma(nrow), dma(nrep), dma(nrep), dma(ncol), dma(ncol),
             dma(nrep), dma(nrep), dma(ncol), dma(ncol), dma(nrep), dma(nrep),
         ],
@@ -440,7 +415,7 @@
             collective_id=0, has_side_effects=True, vmem_limit_bytes=GRANT
         ),
         name="factors",
-    )(activations, out_grads, error_buffer, right_factor.T)
+    )(*(pltpu.with_memory_space_constraint(x, pltpu.HBM) for x in (activations, out_grads, error_buffer, right_factor.T)))
     steps = 8
     new_error, new_right = pl.pallas_call(
         finish_kernel,

time: 42.6 us -> 36 us (0.85)
  local copies, waits for them, and re-layouts: 5.12 us -> 0 us
  Pallas kernels: 36.6 us -> 35.2 us
    unnamed x8 -> x0, local copies, waits for them, and re-layouts: 5.12 us -> none
    pallas_call x1, Pallas kernels: 33.4 us -> 32 us  [kernel_body(): pl.pallas_call(functools.partial(factor_kernel, nrep, nrow, ncol, owners,...]
where the time goes in v3:
time: 36 us; the launch traced here: 35.8 us
  Pallas kernels  35.2 us (98%)
  between operations  0.64 us (2%)
    pallas_call x1, Pallas kernels, kernel_body(): pl.pallas_call(functools.partial(factor_kernel, nrep, nrow, ncol, owners,...  32 us
    pallas_call x1, Pallas kernels, kernel_body(): pl.pallas_call(finish_kernel, out_shape=(jax.ShapeDtypeStruct((rows, cols...  3.15 us

profile of v3, /device:TPU:0, one launch (start us, length us, event | category | flops | bytes accessed | tf_op | source)
XLA Modules:
  0.0 35.8 jit_solution(13675734827006911701)
XLA Ops:
  0.6 32.0 %factors.1 = (f32[1024,1152]{1,0:T(8,128)S(1)}, bf16[48,1024]{1,0:T(8,128)(2,1)S(1)}, bf16[48,1152]{1,0:T(8,128)(2,1)S(1)}, f32[16,1152]{1,0:T(8,128)S(1)}) custom-call(bf16[128,1024]{1,0:T(8,128)(2,1)} %acts_in.1, bf16[128,1152]{1,0:T(8,128)(2,1)} %grads_in.1, f32[1024,1152]{1,0:T(8,128)} %err.1, f32[16,1152]{1,0:T(8,128)} %bitcast.2), custom_call_target="tpu_custom_call" | custom-call | tf_op jit(solution)/shard_map/factors/pallas_call | solution.py:379
  32.7 3.1 %finish.1 = (f32[1024,1152]{1,0:T(8,128)}, f32[16,1152]{1,0:T(8,128)}) custom-call(f32[1024,1152]{1,0:T(8,128)S(1)} %get-tuple-element.8.t, bf16[48,1024]{1,0:T(8,128)(2,1)S(1)} %get-tuple-element.9.los, bf16[48,1152]{1,0:T(8,128)(2,1)S(1)} %get-tuple-element.10.nrs, f32[16,1152]{1,0:T(8,128)S(1)} %get-tuple-element.11.nrt), custom_call_target="tpu_custom_call" | custom-call | tf_op jit(solution)/shard_map/finish/pallas_call | solution.py:420
